TPU v7x, 32 devices: a whole 2x2x4 slice. The times are simulated.
32 devices in a mesh: gx: 4 (over y, x), gy: 4 (over z), gz: 2 (over core).
Axes of the slice: x: 2, y: 2, z: 4, core: 2. Of those that a mesh axis runs over, the one named last changes fastest.
Arguments:
- nodal_scalar_values: float32 [3, 32, 32, 4096], P(None, 'gx', 'gy', 'gz'), may hold values from -6 to 6
- geometry: float32 [6, 4, 4, 512], P(None, 'gx', 'gy', 'gz'), may hold values from -1.2 to 4, as said below
Outputs:
- assembled: float32 [3, 32, 32, 4096], P(None, 'gx', 'gy', 'gz')
Inputs may be any that keep to these rules, and one draw needn't show every extreme that they name: `geometry`: G00, G11 and G22 are positive; each off-diagonal factor is at most 0.3 times the root of the product of its two diagonal factors in magnitude.
All inputs are finite; a program needn't handle non-finite values.
Results may differ from a plain program's by a relative error of at most 0.00007.
Values sent between devices are 32-bit elements; how exact they have to be, the bound alone decides.
A program may use at most 64 MiB of HBM per device.

v0:
```python
import math

import jax
import jax.numpy as jnp
import numpy as np
from jax import lax
from jax.sharding import PartitionSpec as P

interior_points = [
    -0.8717401485096066,
    -0.5917001814331423,
    -0.2092992179024789,
    0.2092992179024789,
    0.5917001814331423,
    0.8717401485096066,
]


def shifted(array, axis, by):
    count = lax.axis_size(axis)
    pairs = [(i, i + by) for i in range(count) if 0 <= i + by < count]
    return lax.ppermute(array, axis, pairs)


def legendre_seven(point):
    previous = 1.0
    current = point
    for order in range(1, 7):
        following = ((2 * order + 1) * point * current - order * previous) / (order + 1)
        previous = current
        current = following
    return current


def gll_tables():
    degree = 7
    points = [-1.0] + interior_points + [1.0]
    values = [legendre_seven(point) for point in points]
    node_count = degree + 1
    weights = np.array([2.0 / (degree * (degree + 1) * value * value) for value in values])
    derivative = np.zeros((node_count, node_count))
    for row_index in range(node_count):
        for col_index in range(node_count):
            if row_index != col_index:
                derivative[row_index, col_index] = values[row_index] / (
                    values[col_index] * (points[row_index] - points[col_index])
                )
    derivative[0, 0] = -degree * (degree + 1) / 4.0
    derivative[node_count - 1, node_count - 1] = degree * (degree + 1) / 4.0
    return (derivative, weights)


def apply_axis(field_in, matrix, direction):
    length = field_in.shape[direction]
    block_size = math.gcd(length, 128)
    big_table = jnp.kron(jnp.eye(block_size // 8, dtype=jnp.float32), matrix)
    dim_list = list(field_in.shape)
    folded_shape = (
        dim_list[:direction] + [length // block_size, block_size] + dim_list[direction + 1 :]
    )
    folded_field = field_in.reshape(folded_shape)
    patterns = ["nbyz,ab->nayz", "xnbz,ab->xnaz", "xynb,ab->xyna"]
    result = jnp.einsum(
        patterns[direction], folded_field, big_table, precision=lax.Precision.HIGHEST
    )
    return result.reshape(field_in.shape)


def expand(field_component, target):
    elem_x, elem_y, elem_z = field_component.shape
    spread = jnp.broadcast_to(
        field_component[:, None, :, None, :, None], (elem_x, 8, elem_y, 8, elem_z, 8)
    )
    return spread.reshape(target)


def stiffness(field_in, geometry):
    derivative, weights = gll_tables()
    matrix = jnp.asarray(derivative, jnp.float32)
    weight_row = jnp.asarray(weights, jnp.float32)
    size_x, size_y, size_z = field_in.shape
    weight_x = jnp.tile(weight_row, size_x // 8)
    weight_y = jnp.tile(weight_row, size_y // 8)
    weight_z = jnp.tile(weight_row, size_z // 8)
    node_weight = weight_x[:, None, None] * weight_y[None, :, None] * weight_z[None, None, :]
    grad_x = apply_axis(field_in, matrix, 0)
    grad_y = apply_axis(field_in, matrix, 1)
    grad_z = apply_axis(field_in, matrix, 2)
    factors = [expand(geometry[index], field_in.shape) for index in range(6)]
    flux_x = node_weight * (factors[0] * grad_x + factors[3] * grad_y + factors[4] * grad_z)
    flux_y = node_weight * (factors[3] * grad_x + factors[1] * grad_y + factors[5] * grad_z)
    flux_z = node_weight * (factors[4] * grad_x + factors[5] * grad_y + factors[2] * grad_z)
    transposed = matrix.T
    return (
        apply_axis(flux_x, transposed, 0)
        + apply_axis(flux_y, transposed, 1)
        + apply_axis(flux_z, transposed, 2)
    )


def combine(middle, below_plane, above_plane, direction):
    length = middle.shape[direction]
    from_above = jnp.concatenate(
        [lax.slice_in_dim(middle, 1, length, axis=direction), above_plane], axis=direction
    )
    from_below = jnp.concatenate(
        [below_plane, lax.slice_in_dim(middle, 0, length - 1, axis=direction)], axis=direction
    )
    position = lax.broadcasted_iota(jnp.int32, middle.shape, direction) % 8
    return (
        middle
        + jnp.where(position == 7, from_above, 0.0)
        + jnp.where(position == 0, from_below, 0.0)
    )


def edge_planes(summed, direction):
    length = summed.shape[direction]
    first_plane = lax.slice_in_dim(summed, 0, 1, axis=direction)
    last_plane = lax.slice_in_dim(summed, length - 1, length, axis=direction)
    return (first_plane, last_plane)


def local(nodal_scalar_values, geometry):
    component_count = nodal_scalar_values.shape[0]
    local_terms = jnp.stack(
        [
            stiffness(nodal_scalar_values[component], geometry)
            for component in range(component_count)
        ]
    )
    summed = local_terms
    first_plane, last_plane = edge_planes(summed, 1)
    below_plane = shifted(last_plane, "gx", 1)
    above_plane = shifted(first_plane, "gx", -1)
    summed = combine(summed, below_plane, above_plane, 1)
    first_plane, last_plane = edge_planes(summed, 2)
    below_plane = shifted(last_plane, "gy", 1)
    above_plane = shifted(first_plane, "gy", -1)
    summed = combine(summed, below_plane, above_plane, 2)
    first_plane, last_plane = edge_planes(summed, 3)
    below_plane = shifted(last_plane, "gz", 1)
    above_plane = shifted(first_plane, "gz", -1)
    summed = combine(summed, below_plane, above_plane, 3)
    return summed


def solution(mesh):
    return jax.shard_map(
        local,
        mesh=mesh,
        in_specs=(P(None, "gx", "gy", "gz"), P(None, "gx", "gy", "gz")),
        out_specs=P(None, "gx", "gy", "gz"),
        check_vma=False,
    )
```

profile of v0, /device:TPU:29, one launch (start us, length us, event | category | flops | bytes accessed | tf_op | source)
XLA Modules:
  0.0 71.7 jit_solution(6164323234273313874)
XLA Ops:
  0.0 1.6 %fusion.134 = (f32[1,8,8,2048]{3,2,1,0:T(8,128)S(1)}, f32[1,8,8,2048]{3,2,1,0:T(8,128)S(1)}, f32[1,8,8,2048]{3,2,1,0:T(8,128)S(1)}) fusion(f32[3,8,8,2048]{3,2,1,0:T(8,128)} %param.8), kind=kLoop, calls=%fused_computation.185 | loop fusion | bytes 3145728 | tf_op jit(solution)/shard_map/slice | solution.py:128
  1.6 0.3 copy-done.4
  1.9 0.6 fusion.18
  2.5 0.6 fusion.22
  3.0 0.6 fusion.20
  3.6 0.8 %fusion.32 = f32[8,8,2048]{2,0,1:T(8,128)S(1)} fusion(f32[8,8,1]{1,0,2:T(8,128)S(1)} %copy-done.12, f32[1,8,8,2048]{3,2,1,0:T(8,128)S(1)} %get-tuple-element.19), kind=kOutput, calls=%fused_computation.64 | convolution fusion | flops 12582912 | bytes 1048832 | tf_op jit(solution)/shard_map/nbyz,ab->nayz/dot_general | solution.py:63
  4.4 1.6 %copy_bitcast_fusion = (f32[8,8,16,128]{3,0,2,1:T(8,128)}, f32[8,8,16,128]{3,0,2,1:T(8,128)}) fusion(f32[1,8,8,2048]{3,2,1,0:T(8,128)S(1)} %get-tuple-element.19, f32[1,8,8,2048]{3,2,1,0:T(8,128)S(1)} %get-tuple-element.18), kind=kLoop, calls=%fused_computation.111 | loop fusion | bytes 2097152 | tf_op jit(solution)/shard_map/reshape;squeeze | solution.py:61
  6.1 0.8 %fusion.42 = f32[8,8,2048]{2,0,1:T(8,128)S(1)} fusion(f32[8,8,1]{1,0,2:T(8,128)S(1)} %copy-done.12, f32[1,8,8,2048]{3,2,1,0:T(8,128)S(1)} %get-tuple-element.18), kind=kOutput, calls=%fused_computation.78 | convolution fusion | flops 12582912 | bytes 1048832 | tf_op jit(solution)/shard_map/nbyz,ab->nayz/dot_general | solution.py:63
  6.9 1.5 %broadcast_multiply_fusion = (f32[16,8,16,8]{3,2,1,0:T(8,128)}, f32[16,8,16,8]{3,2,1,0:T(8,128)}) fusion(f32[8,8]{1,0:T(8,128)S(1)} %copy-done.15, f32[16,16]{1,0:T(8,128)S(1)} %fusion.123, f32[8,8]{1,0:T(8,128)S(1)} %copy-done.16), kind=kLoop, calls=%fused_computation.107 | loop fusion | flops 32768 | bytes 132608 | tf_op jit(solution)/shard_map/jit(kron)/mul | solution.py:56
  8.4 1.6 %reshape.403 = f32[128,128,1,1]{1,0,2,3:T(8,128)S(1)} reshape(f32[16,8,16,8]{3,2,1,0:T(8,128)} %get-tuple-element.24) | data formatting | bytes 131072 | tf_op jit(solution)/shard_map/jit(kron)/mul | solution.py:56
  10.2 0.1 broadcast_in_dim.177
  10.4 0.1 broadcast_in_dim.173
  10.6 0.1 broadcast_in_dim.165
  10.9 1.7 %reshape.406 = f32[128,128,1,1]{1,0,2,3:T(8,128)S(1)} reshape(f32[16,8,16,8]{3,2,1,0:T(8,128)} %get-tuple-element.23) | data formatting | bytes 131072 | tf_op jit(solution)/shard_map/jit(kron)/mul | solution.py:56
  12.6 0.3 copy.189
  12.9 2.4 %convolution_bitcast_fusion.3 = f32[8,8,16,128]{3,2,1,0:T(8,128)} fusion(f32[8,8,16,128]{3,0,2,1:T(8,128)} %get-tuple-element.32, f32[128,128,1,1]{1,0,2,3:T(8,128)S(1)} %reshape.403), kind=kOutput, calls=%fused_computation.40 | convolution fusion | flops 201326592 | bytes 1114112 | tf_op jit(solution)/shard_map/xynb,ab->xyna/dot_general | solution.py:63
  15.3 0.6 convolution_bitcast_fusion.5
  16.4 1.6 %convolution_bitcast_fusion.4 = f32[8,8,16,128]{3,2,1,0:T(8,128)S(1)} fusion(f32[8,8,16,128]{3,0,2,1:T(8,128)} %get-tuple-element.33, f32[128,128,1,1]{1,0,2,3:T(8,128)S(1)} %reshape.403), kind=kOutput, calls=%fused_computation.41 | convolution fusion | flops 201326592 | bytes 1114112 | tf_op jit(solution)/shard_map/xynb,ab->xyna/dot_general | solution.py:63
  18.0 3.2 %convolution_bitcast_fusion = f32[8,8,2048]{2,0,1:T(8,128)} fusion(f32[8,8,2048]{2,0,1:T(8,128)S(1)} %fusion.32, f32[8,8,16,128]{3,2,1,0:T(8,128)} %convolution_bitcast_fusion.3, f32[8,8,2048]{2,0,1:T(8,128)S(1)} %fusion.18, f32[2048]{0:T(1024)S(1)} %broadcast_in_dim.177, f32[2048]{0:T(1024)S(1)} %broadcast_in_dim.173, f32[2048]{0:T(1024)S(1)} %broadcast_in_dim.165, ...), kind=kOutput, calls=%fused_computation.18 | convolution fusion | flops 202244096 | bytes 2195712 | tf_op jit(solution)/shard_map/xynb,ab->xyna/dot_general | solution.py:63
  21.2 2.0 %convolution_bitcast_fusion.1 = f32[8,8,2048]{2,0,1:T(8,128)} fusion(f32[8,8,2048]{2,0,1:T(8,128)S(1)} %fusion.42, f32[8,8,16,128]{3,2,1,0:T(8,128)S(1)} %convolution_bitcast_fusion.4, f32[8,8,2048]{2,0,1:T(8,128)S(1)} %fusion.20, f32[2048]{0:T(1024)S(1)} %broadcast_in_dim.177, f32[2048]{0:T(1024)S(1)} %broadcast_in_dim.173, ...), kind=kOutput, calls=%fused_computation.19 | convolution fusion | flops 202244096 | bytes 2195712 | tf_op jit(solution)/shard_map/xynb,ab->xyna/dot_general | solution.py:63
  23.2 4.0 %multiply_multiply_fusion.7 = (f32[8,8,2048]{2,0,1:T(8,128)}, f32[8,8,2048]{2,0,1:T(8,128)}, f32[8,8,2048]{2,0,1:T(8,128)S(1)}, f32[8,8,2048]{2,0,1:T(8,128)}) fusion(f32[8,8,16,128]{3,2,1,0:T(8,128)S(1)} %convolution_bitcast_fusion.5, f32[8,8,2048]{2,0,1:T(8,128)S(1)} %fusion.22, f32[2048]{0:T(1024)S(1)} %broadcast_in_dim.173, ...), kind=kOutput, calls=%fused_computation.7 | convolution fusion | flops 15073280 | bytes 6849024 | tf_op jit(solution)/shard_map/nbyz,ab->nayz/dot_general | solution.py:63
  27.2 1.6 %fusion.54 = f32[8,8,2048]{2,0,1:T(8,128)} fusion(f32[8,8,1]{1,0,2:T(8,128)S(1)} %copy-done.12, f32[8,8,2048]{2,0,1:T(8,128)S(1)} %get-tuple-element.22), kind=kOutput, calls=%fused_computation.94 | convolution fusion | flops 12582912 | bytes 1048832 | tf_op jit(solution)/shard_map/xnbz,ab->xnaz/dot_general | solution.py:63
  29.0 1.9 %fusion.57 = f32[8,8,2048]{2,0,1:T(8,128)S(1)} fusion(f32[8,8,1]{1,0,2:T(8,128)S(1)} %copy-done.12, f32[8,8,2048]{2,0,1:T(8,128)} %get-tuple-element.21), kind=kOutput, calls=%fused_computation.97 | convolution fusion | flops 12582912 | bytes 1048832 | tf_op jit(solution)/shard_map/xnbz,ab->xnaz/dot_general | solution.py:63
  31.0 2.3 %convolution_bitcast_fusion.2 = f32[8,8,2048]{2,0,1:T(8,128)S(1)} fusion(f32[8,8,2048]{2,0,1:T(8,128)} %get-tuple-element.31, f32[8,8,16,128]{3,2,1,0:T(8,128)S(1)} %convolution_bitcast_fusion.5, f32[8,8,2048]{2,0,1:T(8,128)S(1)} %fusion.22, f32[2048]{0:T(1024)S(1)} %broadcast_in_dim.177, f32[2048]{0:T(1024)S(1)} %broadcast_in_dim.173, ...), kind=kOutput, calls=%fused_computation.20 | convolution fusion | flops 202244096 | bytes 2195712 | tf_op jit(solution)/shard_map/xynb,ab->xyna/dot_general | solution.py:63
  33.3 0.8 %fusion.60 = f32[8,8,2048]{2,0,1:T(8,128)S(1)} fusion(f32[8,8,1]{1,0,2:T(8,128)S(1)} %copy-done.12, f32[8,8,2048]{2,0,1:T(8,128)S(1)} %copy-done.11), kind=kOutput, calls=%fused_computation.100 | convolution fusion | flops 12582912 | bytes 1048832 | tf_op jit(solution)/shard_map/xnbz,ab->xnaz/dot_general | solution.py:63
  34.2 1.5 %fusion.5 = f32[1,8,8,2048]{3,1,2,0:T(8,128)S(1)} fusion(f32[8,8,2048]{2,0,1:T(8,128)S(1)} %copy-done.10, f32[8,8,1]{1,0,2:T(8,128)S(1)} %copy-done.12, f32[8,8,2048]{2,0,1:T(8,128)S(1)} %copy-done.8, f32[8,8,2048]{2,0,1:T(8,128)S(1)} %fusion.32, f32[8,8,16,128]{3,2,1,0:T(8,128)S(1)} %copy-done.1, f32[8,8,2048]{2,0,1:T(8,128)S(1)} %fusion.18, ...), kind=kOutput, calls=%fused_computation.17 | convolution fusion | flops 13762560 | bytes 3179008 | tf_op jit(solution)/shard_map/nbyz,ab->nayz/dot_general | solution.py:63
  35.7 1.4 %fusion.4 = f32[1,8,8,2048]{3,1,2,0:T(8,128)S(1)} fusion(f32[8,8,2048]{2,0,1:T(8,128)S(1)} %copy-done.9, f32[8,8,1]{1,0,2:T(8,128)S(1)} %copy-done.12, f32[8,8,2048]{2,0,1:T(8,128)S(1)} %fusion.57, f32[8,8,2048]{2,0,1:T(8,128)S(1)} %fusion.42, f32[8,8,16,128]{3,2,1,0:T(8,128)S(1)} %copy-done.3, f32[8,8,2048]{2,0,1:T(8,128)S(1)} %fusion.20, ...), kind=kOutput, calls=%fused_computation.16 | convolution fusion | flops 13762560 | bytes 3179008 | tf_op jit(solution)/shard_map/nbyz,ab->nayz/dot_general | solution.py:63
  37.2 1.4 %fusion.3 = f32[1,8,8,2048]{3,1,2,0:T(8,128)S(1)} fusion(f32[8,8,2048]{2,0,1:T(8,128)S(1)} %convolution_bitcast_fusion.2, f32[8,8,1]{1,0,2:T(8,128)S(1)} %copy-done.12, f32[8,8,2048]{2,0,1:T(8,128)S(1)} %fusion.60, f32[8,8,2048]{2,0,1:T(8,128)S(1)} %copy-done.5, f32[8,8,16,128]{3,2,1,0:T(8,128)S(1)} %convolution_bitcast_fusion.5, ...), kind=kOutput, calls=%fused_computation.15 | convolution fusion | flops 13762560 | bytes 3179008 | tf_op jit(solution)/shard_map/nbyz,ab->nayz/dot_general | solution.py:63
  38.6 0.1 pad_maximum_fusion
  38.8 0.3 fusion.132
  39.0 3.1 %collective-permute-start = (f32[3,1,8,2048]{3,1,2,0:T(1,128)S(1)}, f32[3,1,8,2048]{3,1,2,0:T(1,128)S(1)}, u32[]{:S(2)}, u32[]{:S(2)}) collective-permute-start(f32[3,1,8,2048]{3,1,2,0:T(1,128)S(1)} %get-tuple-element.14), channel_id=1, source_target_pairs={{8,0},{16,8},{24,16},{9,1},{17,9},{25,17},{10,2},{18,10},{26,18},{... | collective-permute-start | bytes 589832 | tf_op jit(solution)/shard_map/ppermute | solution.py:22
  42.1 2.2 %collective-permute-start.1 = (f32[3,1,8,2048]{3,1,2,0:T(1,128)S(1)}, f32[3,1,8,2048]{3,1,2,0:T(1,128)S(1)}, u32[]{:S(2)}, u32[]{:S(2)}) collective-permute-start(f32[3,1,8,2048]{3,1,2,0:T(1,128)S(1)} %get-tuple-element.13), channel_id=1, source_target_pairs={{0,8},{8,16},{16,24},{1,9},{9,17},{17,25},{2,10},{10,18},{18,26},{... | collective-permute-start | bytes 589832 | tf_op jit(solution)/shard_map/ppermute | solution.py:22
  44.4 0.4 fusion.133
  44.8 2.0 %collective-permute-done = f32[3,1,8,2048]{3,1,2,0:T(1,128)S(1)} collective-permute-done((f32[3,1,8,2048]{3,1,2,0:T(1,128)S(1)}, f32[3,1,8,2048]{3,1,2,0:T(1,128)S(1)}, u32[]{:S(2)}, u32[]{:S(2)}) %collective-permute-start) | collective-permute-done | bytes 196640 | tf_op jit(solution)/shard_map/ppermute | solution.py:22
  46.7 4.1 %collective-permute-done.1 = f32[3,1,8,2048]{3,1,2,0:T(1,128)S(1)} collective-permute-done((f32[3,1,8,2048]{3,1,2,0:T(1,128)S(1)}, f32[3,1,8,2048]{3,1,2,0:T(1,128)S(1)}, u32[]{:S(2)}, u32[]{:S(2)}) %collective-permute-start.1) | collective-permute-done | bytes 196640 | tf_op jit(solution)/shard_map/ppermute | solution.py:22
  50.8 0.8 %fusion.7 = f32[3,8,8,2048]{3,1,2,0:T(8,128)S(1)} fusion(f32[3,1,8,2048]{3,1,2,0:T(1,128)S(1)} %collective-permute-done, f32[3,7,8,2048]{3,1,2,0:T(8,128)S(1)} %get-tuple-element.16, f32[3,7,8,2048]{3,1,2,0:T(8,128)S(1)} %get-tuple-element.15, f32[3,1,8,2048]{3,1,2,0:T(1,128)S(1)} %collective-permute-done.1, s32[8]{0:T(128)S(1)} %get-tuple-element.34, ...), kind=kLoop, calls=%fused_computation.30 | loop fusion | flops 4325376 | bytes 6291528 | tf_op jit(solution)/shard_map/add | solution.py:111
  51.6 2.1 %collective-permute-start.2 = (f32[3,8,1,2048]{3,1,2,0:T(8,128)S(1)}, f32[3,8,1,2048]{3,1,2,0:T(8,128)S(1)}, u32[]{:S(2)}, u32[]{:S(2)}) collective-permute-start(f32[3,8,1,2048]{3,1,2,0:T(8,128)S(1)} %get-tuple-element.10), channel_id=1, source_target_pairs={{2,0},{4,2},{6,4},{3,1},{5,3},{7,5},{10,8},{12,10},{14,12},{11,9},... | collective-permute-start | bytes 589832 | tf_op jit(solution)/shard_map/ppermute | solution.py:22
  53.7 1.3 %collective-permute-start.3 = (f32[3,8,1,2048]{3,1,2,0:T(8,128)S(1)}, f32[3,8,1,2048]{3,1,2,0:T(8,128)S(1)}, u32[]{:S(2)}, u32[]{:S(2)}) collective-permute-start(f32[3,8,1,2048]{3,1,2,0:T(8,128)S(1)} %get-tuple-element.9), channel_id=1, source_target_pairs={{0,2},{2,4},{4,6},{1,3},{3,5},{5,7},{8,10},{10,12},{12,14},{9,11},... | collective-permute-start | bytes 589832 | tf_op jit(solution)/shard_map/ppermute | solution.py:22
  55.0 0.3 fusion.131
  55.4 1.0 %collective-permute-done.2 = f32[3,8,1,2048]{3,1,2,0:T(8,128)S(1)} collective-permute-done((f32[3,8,1,2048]{3,1,2,0:T(8,128)S(1)}, f32[3,8,1,2048]{3,1,2,0:T(8,128)S(1)}, u32[]{:S(2)}, u32[]{:S(2)}) %collective-permute-start.2) | collective-permute-done | bytes 196640 | tf_op jit(solution)/shard_map/ppermute | solution.py:22
  56.3 3.8 %collective-permute-done.3 = f32[3,8,1,2048]{3,1,2,0:T(8,128)S(1)} collective-permute-done((f32[3,8,1,2048]{3,1,2,0:T(8,128)S(1)}, f32[3,8,1,2048]{3,1,2,0:T(8,128)S(1)}, u32[]{:S(2)}, u32[]{:S(2)}) %collective-permute-start.3) | collective-permute-done | bytes 196640 | tf_op jit(solution)/shard_map/ppermute | solution.py:22
  60.1 0.5 fusion.9
  60.7 5.0 %collective-permute-start.4 = (f32[3,8,8,1]{3,1,2,0:T(8,128)S(1)}, f32[3,8,8,1]{3,1,2,0:T(8,128)S(1)}, u32[]{:S(2)}, u32[]{:S(2)}) collective-permute-start(f32[3,8,8,1]{3,1,2,0:T(8,128)S(1)} %get-tuple-element.6), channel_id=1, source_target_pairs={{1,0},{3,2},{5,4},{7,6},{9,8},{11,10},{13,12},{15,14},{17,16},{19,... | collective-permute-start | bytes 2312 | tf_op jit(solution)/shard_map/ppermute | solution.py:22
  65.7 1.3 %collective-permute-start.5 = (f32[3,8,8,1]{3,1,2,0:T(8,128)S(1)}, f32[3,8,8,1]{3,1,2,0:T(8,128)S(1)}, u32[]{:S(2)}, u32[]{:S(2)}) collective-permute-start(f32[3,8,8,1]{3,1,2,0:T(8,128)S(1)} %get-tuple-element.5), channel_id=1, source_target_pairs={{0,1},{2,3},{4,5},{6,7},{8,9},{10,11},{12,13},{14,15},{16,17},{18,... | collective-permute-start | bytes 2312 | tf_op jit(solution)/shard_map/ppermute | solution.py:22
  67.0 0.6 fusion.129
  67.6 1.3 %collective-permute-done.5 = f32[3,8,8,1]{3,1,2,0:T(8,128)S(1)} collective-permute-done((f32[3,8,8,1]{3,1,2,0:T(8,128)S(1)}, f32[3,8,8,1]{3,1,2,0:T(8,128)S(1)}, u32[]{:S(2)}, u32[]{:S(2)}) %collective-permute-start.5) | collective-permute-done | bytes 800 | tf_op jit(solution)/shard_map/ppermute | solution.py:22
  68.9 0.7 fusion.11
  69.6 2.1 %copy.76 = f32[3,8,8,2048]{3,2,1,0:T(8,128)} copy(f32[3,8,8,2048]{3,1,2,0:T(8,128)S(1)} %fusion.11) | data formatting | bytes 3145728 | tf_op jit(solution)/shard_map/add | solution.py:111
  (54 shorter events, 1.3 us)
Async XLA Ops:
  0.0 1.9 %copy-start.4 = (f32[3,8,8,2048]{3,2,1,0:T(8,128)S(1)}, f32[3,8,8,2048]{3,2,1,0:T(8,128)}, u32[]{:S(2)}) copy-start(f32[3,8,8,2048]{3,2,1,0:T(8,128)} %param.8) | copy-start | bytes 4718596
  0.0 1.9 %copy-start.12 = (f32[8,8,1]{1,0,2:T(8,128)S(1)}, f32[8,8,1]{1,0,2:T(8,128)}, u32[]{:S(2)}) copy-start(f32[8,8,1]{1,0,2:T(8,128)} %constant.39) | copy-start | bytes 772
  1.9 10.7 %copy-start.6 = (f32[1,8,8,2048]{3,2,1,0:T(8,128)}, f32[1,8,8,2048]{3,2,1,0:T(8,128)S(1)}, u32[]{:S(2)}) copy-start(f32[1,8,8,2048]{3,2,1,0:T(8,128)S(1)} %get-tuple-element.17) | copy-start | bytes 1572868
  4.4 2.5 %copy-start.15 = (f32[8,8]{1,0:T(8,128)S(1)}, f32[8,8]{1,0:T(8,128)}, u32[]{:S(2)}) copy-start(f32[8,8]{1,0:T(8,128)} %constant.38) | copy-start | bytes 772
  4.4 2.4 %copy-start.16 = (f32[8,8]{1,0:T(8,128)S(1)}, f32[8,8]{1,0:T(8,128)}, u32[]{:S(2)}) copy-start(f32[8,8]{1,0:T(8,128)} %constant.35.clone) | copy-start | bytes 772
  6.9 3.2 %copy-start.13 = (f32[6,1,1,256]{3,2,1,0:T(1,128)S(1)}, f32[6,1,1,256]{3,2,1,0:T(1,128)}, u32[]{:S(2)}) copy-start(f32[6,1,1,256]{3,2,1,0:T(1,128)} %param.9) | copy-start | bytes 18436
  6.9 3.8 %copy-start.14 = (f32[8]{0:T(128)S(1)}, f32[8]{0:T(128)}, u32[]{:S(2)}) copy-start(f32[8]{0:T(128)} %constant.36.clone) | copy-start | bytes 100
  18.0 5.2 %copy-start.2 = (f32[8,8,16,128]{3,2,1,0:T(8,128)}, f32[8,8,16,128]{3,2,1,0:T(8,128)S(1)}, u32[]{:S(2)}) copy-start(f32[8,8,16,128]{3,2,1,0:T(8,128)S(1)} %convolution_bitcast_fusion.4) | copy-start | bytes 1572868
  21.2 2.0 %copy-start = (f32[8,8,16,128]{3,2,1,0:T(8,128)S(1)}, f32[8,8,16,128]{3,2,1,0:T(8,128)}, u32[]{:S(2)}) copy-start(f32[8,8,16,128]{3,2,1,0:T(8,128)} %convolution_bitcast_fusion.3) | copy-start | bytes 1572868
  21.2 2.0 %copy-start.7 = (f32[1,8,8,2048]{3,2,1,0:T(8,128)S(1)}, f32[1,8,8,2048]{3,2,1,0:T(8,128)}, u32[]{:S(2)}) copy-start(f32[1,8,8,2048]{3,2,1,0:T(8,128)} %copy-done.6) | copy-start | bytes 1572868
  29.0 4.3 %copy-start.11 = (f32[8,8,2048]{2,0,1:T(8,128)S(1)}, f32[8,8,2048]{2,0,1:T(8,128)}, u32[]{:S(2)}) copy-start(f32[8,8,2048]{2,0,1:T(8,128)} %get-tuple-element.20) | copy-start | bytes 1572868
  31.0 3.2 %copy-start.1 = (f32[8,8,16,128]{3,2,1,0:T(8,128)S(1)}, f32[8,8,16,128]{3,2,1,0:T(8,128)}, u32[]{:S(2)}) copy-start(f32[8,8,16,128]{3,2,1,0:T(8,128)} %convolution_bitcast_fusion.3) | copy-start | bytes 1572868
  31.0 3.2 %copy-start.8 = (f32[8,8,2048]{2,0,1:T(8,128)S(1)}, f32[8,8,2048]{2,0,1:T(8,128)}, u32[]{:S(2)}) copy-start(f32[8,8,2048]{2,0,1:T(8,128)} %fusion.54) | copy-start | bytes 1572868
  31.0 3.2 %copy-start.10 = (f32[8,8,2048]{2,0,1:T(8,128)S(1)}, f32[8,8,2048]{2,0,1:T(8,128)}, u32[]{:S(2)}) copy-start(f32[8,8,2048]{2,0,1:T(8,128)} %convolution_bitcast_fusion) | copy-start | bytes 1572868
  34.2 1.5 %copy-start.3 = (f32[8,8,16,128]{3,2,1,0:T(8,128)S(1)}, f32[8,8,16,128]{3,2,1,0:T(8,128)}, u32[]{:S(2)}) copy-start(f32[8,8,16,128]{3,2,1,0:T(8,128)} %copy-done.2) | copy-start | bytes 1572868
  34.2 1.5 %copy-start.9 = (f32[8,8,2048]{2,0,1:T(8,128)S(1)}, f32[8,8,2048]{2,0,1:T(8,128)}, u32[]{:S(2)}) copy-start(f32[8,8,2048]{2,0,1:T(8,128)} %convolution_bitcast_fusion.1) | copy-start | bytes 1572868
  35.7 1.5 %copy-start.5 = (f32[8,8,2048]{2,0,1:T(8,128)S(1)}, f32[8,8,2048]{2,0,1:T(8,128)}, u32[]{:S(2)}) copy-start(f32[8,8,2048]{2,0,1:T(8,128)} %get-tuple-element.31) | copy-start | bytes 1572868
  39.0 7.7 %collective-permute-start = (f32[3,1,8,2048]{3,1,2,0:T(1,128)S(1)}, f32[3,1,8,2048]{3,1,2,0:T(1,128)S(1)}, u32[]{:S(2)}, u32[]{:S(2)}) collective-permute-start(f32[3,1,8,2048]{3,1,2,0:T(1,128)S(1)} %get-tuple-element.14), channel_id=1, source_target_pairs={{8,0},{16,8},{24,16},{9,1},{17,9},{25,17},{10,2},{18,10},{26,18},{... | collective-permute-start | bytes 589832 | tf_op jit(solution)/shard_map/ppermute | solution.py:22
  42.1 8.7 %collective-permute-start.1 = (f32[3,1,8,2048]{3,1,2,0:T(1,128)S(1)}, f32[3,1,8,2048]{3,1,2,0:T(1,128)S(1)}, u32[]{:S(2)}, u32[]{:S(2)}) collective-permute-start(f32[3,1,8,2048]{3,1,2,0:T(1,128)S(1)} %get-tuple-element.13), channel_id=1, source_target_pairs={{0,8},{8,16},{16,24},{1,9},{9,17},{17,25},{2,10},{10,18},{18,26},{... | collective-permute-start | bytes 589832 | tf_op jit(solution)/shard_map/ppermute | solution.py:22
  51.6 4.7 %collective-permute-start.2 = (f32[3,8,1,2048]{3,1,2,0:T(8,128)S(1)}, f32[3,8,1,2048]{3,1,2,0:T(8,128)S(1)}, u32[]{:S(2)}, u32[]{:S(2)}) collective-permute-start(f32[3,8,1,2048]{3,1,2,0:T(8,128)S(1)} %get-tuple-element.10), channel_id=1, source_target_pairs={{2,0},{4,2},{6,4},{3,1},{5,3},{7,5},{10,8},{12,10},{14,12},{11,9},... | collective-permute-start | bytes 589832 | tf_op jit(solution)/shard_map/ppermute | solution.py:22
  53.7 6.4 %collective-permute-start.3 = (f32[3,8,1,2048]{3,1,2,0:T(8,128)S(1)}, f32[3,8,1,2048]{3,1,2,0:T(8,128)S(1)}, u32[]{:S(2)}, u32[]{:S(2)}) collective-permute-start(f32[3,8,1,2048]{3,1,2,0:T(8,128)S(1)} %get-tuple-element.9), channel_id=1, source_target_pairs={{0,2},{2,4},{4,6},{1,3},{3,5},{5,7},{8,10},{10,12},{12,14},{9,11},... | collective-permute-start | bytes 589832 | tf_op jit(solution)/shard_map/ppermute | solution.py:22
  60.7 6.8 %collective-permute-start.4 = (f32[3,8,8,1]{3,1,2,0:T(8,128)S(1)}, f32[3,8,8,1]{3,1,2,0:T(8,128)S(1)}, u32[]{:S(2)}, u32[]{:S(2)}) collective-permute-start(f32[3,8,8,1]{3,1,2,0:T(8,128)S(1)} %get-tuple-element.6), channel_id=1, source_target_pairs={{1,0},{3,2},{5,4},{7,6},{9,8},{11,10},{13,12},{15,14},{17,16},{19,... | collective-permute-start | bytes 2312 | tf_op jit(solution)/shard_map/ppermute | solution.py:22
  65.7 3.2 %collective-permute-start.5 = (f32[3,8,8,1]{3,1,2,0:T(8,128)S(1)}, f32[3,8,8,1]{3,1,2,0:T(8,128)S(1)}, u32[]{:S(2)}, u32[]{:S(2)}) collective-permute-start(f32[3,8,8,1]{3,1,2,0:T(8,128)S(1)} %get-tuple-element.5), channel_id=1, source_target_pairs={{0,1},{2,3},{4,5},{6,7},{8,9},{10,11},{12,13},{14,15},{16,17},{18,... | collective-permute-start | bytes 2312 | tf_op jit(solution)/shard_map/ppermute | solution.py:22
where the time goes:
time: 72.1 us; the launch traced here: 71.7 us
  matrix products  28.2 us (39%)
  starting transfers between devices  14.9 us (21%)
  local copies, waits for them, and re-layouts  12.2 us (17%)
  waiting for transfers between devices  12.1 us (17%)
  other arithmetic  3.76 us (5%)
    dot_general x18, matrix products, apply_axis(): jnp.einsum(patterns[direction], folded_field, big_table, precision=lax.Pr...  28.2 us
    ppermute x6, starting transfers between devices, shifted(): return lax.ppermute(array, axis, pairs)  14.9 us
    ppermute x6, waiting for transfers between devices, shifted(): return lax.ppermute(array, axis, pairs)  12.1 us
    mul x2, local copies, waits for them, and re-layouts, apply_axis(): big_table = jnp.kron(jnp.eye(block_size // 8, dtype=jnp.float32), matrix)  3.3 us
    add x1, local copies, waits for them, and re-layouts, combine(): middle + jnp.where(position == 7, from_above, 0.0)  2.06 us
    add x3, other arithmetic, combine(): middle + jnp.where(position == 7, from_above, 0.0)  2 us
    another operation x1, local copies, waits for them, and re-layouts, apply_axis(): folded_field = field_in.reshape(folded_shape)  1.61 us
    slice x1, local copies, waits for them, and re-layouts, local(): nodal_scalar_values[component]  1.58 us
  transfers between devices with their start and end apart: 6, of which 5 were waited for; matrix products, arithmetic and copies ran while one was open for 2% of the time, Pallas kernels for 0%

commit v1 on v0

v1 whole, which is shorter than its diff:
```python
import functools

import jax
import jax.numpy as jnp
import numpy as np
from jax import lax
from jax.experimental import pallas as pl
from jax.experimental.pallas import tpu as pltpu
from jax.sharding import PartitionSpec as P

interior_points = [
    -0.8717401485096066,
    -0.5917001814331423,
    -0.2092992179024789,
    0.2092992179024789,
    0.5917001814331423,
    0.8717401485096066,
]
MESH = pl.DeviceIdType.MESH
STEP = 256
LANES = 128


def legendre_seven(point):
    previous = 1.0
    current = point
    for order in range(1, 7):
        following = ((2 * order + 1) * point * current - order * previous) / (order + 1)
        previous = current
        current = following
    return current


def gll_tables():
    degree = 7
    points = [-1.0] + interior_points + [1.0]
    values = [legendre_seven(point) for point in points]
    node_count = degree + 1
    weights = np.array([2.0 / (degree * (degree + 1) * value * value) for value in values])
    derivative = np.zeros((node_count, node_count))
    for row_index in range(node_count):
        for col_index in range(node_count):
            if row_index != col_index:
                derivative[row_index, col_index] = values[row_index] / (
                    values[col_index] * (points[row_index] - points[col_index])
                )
    derivative[0, 0] = -degree * (degree + 1) / 4.0
    derivative[node_count - 1, node_count - 1] = degree * (degree + 1) / 4.0
    return (derivative, weights)


def halves(table):
    table = np.asarray(table, np.float32)
    high = table.astype(jnp.bfloat16)
    low = (table - high.astype(np.float32)).astype(jnp.bfloat16)
    return high, low


def tables():
    derivative, weights = gll_tables()
    eye = np.eye(8)
    plane_weight = np.kron(weights, weights)
    forward_xy = np.concatenate([np.kron(derivative, eye), np.kron(eye, derivative)], axis=0)
    back_xy = np.concatenate([np.kron(derivative.T, eye), np.kron(eye, derivative.T)], axis=1)
    back_xy = back_xy * np.tile(plane_weight, 2)[None, :]
    forward_z = np.kron(np.eye(16), derivative.T)
    back_z = np.kron(np.eye(16), derivative)
    high, low = halves(forward_xy)
    forward_xy = np.concatenate([high, high, low, low], axis=1)
    high, low = halves(back_xy)
    back_xy = np.concatenate(
        [np.concatenate([high, high], axis=1), np.concatenate([low, low], axis=1)], axis=0
    )
    high, low = halves(forward_z)
    forward_z = np.tile(np.concatenate([high, low], axis=1), (2, 1))
    high, low = halves(back_z)
    back_z = np.tile(np.concatenate([high, low], axis=1), (2, 1))
    matrices = np.concatenate([forward_xy, back_xy, forward_z, back_z], axis=0)
    plane = np.repeat(plane_weight[:, None], LANES, axis=1)
    along = np.repeat(np.tile(weights, LANES // 8)[None, :], 8, axis=0)
    scales = np.concatenate([plane, along], axis=0).astype(np.float32)
    return matrices, scales


def split(value):
    high = value.astype(jnp.bfloat16)
    low = (value - high.astype(jnp.float32)).astype(jnp.bfloat16)
    return high, low


def product(left, right):
    return jnp.dot(left, right, preferred_element_type=jnp.float32)


def along_lanes(high, low, table):
    pieces = []
    for start in range(0, high.shape[1], LANES):
        both = jnp.concatenate(
            [high[:, start : start + LANES], low[:, start : start + LANES]], axis=1
        )
        twice = product(both, table)
        pieces.append(twice[:, :LANES] + twice[:, LANES:])
    return jnp.concatenate(pieces, axis=1)


def kernel(
    sizes,
    chunk,
    u_hbm,
    geo_hbm,
    mat_hbm,
    scale_hbm,
    out,
    u,
    geo,
    mat,
    scale,
    metric,
    local,
    y_out,
    x_in,
    y_in,
    corner_out,
    corner_in,
    z_out,
    z_in,
    in_sem,
    const_sem,
    x_send,
    x_recv,
    y_send,
    y_recv,
    c_send,
    c_recv,
    z_send,
    z_recv,
):
    comps, _, _, total = u.shape
    count = total // chunk
    order = [0] + ([count - 1] if count > 1 else []) + list(range(1, count - 1))
    names = ("gx", "gy", "gz")
    place = {name: lax.axis_index(name) for name in names}
    below = {name: place[name] > 0 for name in names}
    above = {name: place[name] < sizes[name] - 1 for name in names}

    const_copies = [
        pltpu.make_async_copy(mat_hbm, mat, const_sem.at[0]),
        pltpu.make_async_copy(scale_hbm, scale, const_sem.at[1]),
        pltpu.make_async_copy(geo_hbm, geo, const_sem.at[2]),
    ]
    for copy in const_copies:
        copy.start()
    in_copies = {}
    for c in order:
        span = pl.ds(c * chunk, chunk)
        in_copies[c] = pltpu.make_async_copy(
            u_hbm.at[:, :, :, span], u.at[:, :, :, span], in_sem.at[c]
        )
        in_copies[c].start()

    barrier = pltpu.get_barrier_semaphore()
    for name in names:
        for there, by in ((below[name], -1), (above[name], 1)):

            @pl.when(there)
            def _(name=name, by=by):
                pl.semaphore_signal(
                    barrier, inc=1, device_id={name: place[name] + by}, device_id_type=MESH
                )

    for side in range(2):
        there = below if side == 0 else above

        @pl.when(jnp.logical_not(there["gx"]))
        def _(side=side):
            x_in[side] = jnp.zeros(x_in.shape[1:], jnp.float32)

        @pl.when(jnp.logical_not(there["gy"]))
        def _(side=side):
            y_in[side] = jnp.zeros(y_in.shape[1:], jnp.float32)
            corner_in[side] = jnp.zeros(corner_in.shape[1:], jnp.float32)

        @pl.when(jnp.logical_not(there["gz"]))
        def _(side=side):
            z_in[side] = jnp.zeros(z_in.shape[1:], jnp.float32)

    for copy in const_copies:
        copy.wait()

    rows = jnp.concatenate(
        [geo[k, 0] for k in range(6)] + [jnp.zeros((2, geo.shape[-1]), jnp.float32)], axis=0
    )
    lane = lax.broadcasted_iota(jnp.int32, (8, LANES), 1)
    for tile in range(total // LANES):
        first = tile * (LANES // 8)
        block = rows[:, first // LANES * LANES : first // LANES * LANES + LANES]
        spread = jnp.take_along_axis(block, lane // 8 + first % LANES, axis=1)
        metric[:, tile * LANES : (tile + 1) * LANES] = spread * scale[64:72, :]

    def x_copy(side, c):
        span = pl.ds(c * chunk, chunk)
        return pltpu.make_async_remote_copy(
            local.at[:, 7 if side == 0 else 0, :, span],
            x_in.at[side, :, :, span],
            x_send.at[side, c],
            x_recv.at[side, c],
            device_id={"gx": place["gx"] + (1 if side == 0 else -1)},
            device_id_type=MESH,
        )

    def y_copy(side, c):
        span = pl.ds(c * chunk, chunk)
        return pltpu.make_async_remote_copy(
            y_out.at[side, :, :, span],
            y_in.at[side, :, :, span],
            y_send.at[side, c],
            y_recv.at[side, c],
            device_id={"gy": place["gy"] + (1 if side == 0 else -1)},
            device_id_type=MESH,
        )

    def c_copy(side, c):
        span = pl.ds(c * chunk, chunk)
        return pltpu.make_async_remote_copy(
            corner_out.at[side, :, span],
            corner_in.at[side, :, span],
            c_send.at[side, c],
            c_recv.at[side, c],
            device_id={"gy": place["gy"] + (1 if side == 0 else -1)},
            device_id_type=MESH,
        )

    def z_copy(side):
        return pltpu.make_async_remote_copy(
            z_out.at[side],
            z_in.at[side],
            z_send.at[side],
            z_recv.at[side],
            device_id={"gz": place["gz"] + (1 if side == 0 else -1)},
            device_id_type=MESH,
        )

    def target(name, side):
        return above[name] if side == 0 else below[name]

    def source(name, side):
        return below[name] if side == 0 else above[name]

    def when_do(condition, act):
        @pl.when(condition)
        def _():
            act()

    forward_xy, back_xy = mat[0:128, :], mat[128:256, :]
    forward_z, back_z = mat[256:512, :], mat[512:768, :]

    greeted = sum(side[name].astype(jnp.int32) for name in names for side in (below, above))
    for at, c in enumerate(order):
        in_copies[c].wait()
        for start in range(c * chunk, (c + 1) * chunk, STEP):
            lanes = slice(start, start + STEP)
            g00, g11, g22, g01, g02, g12 = [metric[k : k + 1, lanes] for k in range(6)]
            for comp in range(comps):
                field = u[comp, :, :, lanes].reshape(64, STEP)
                high, low = split(field)
                both = product(forward_xy, jnp.concatenate([high, low, high, low], axis=0))
                grad_x, grad_y = both[:64], both[64:]
                grad_z = along_lanes(high, low, forward_z)
                flux_x = g00 * grad_x + g01 * grad_y + g02 * grad_z
                flux_y = g01 * grad_x + g11 * grad_y + g12 * grad_z
                flux_z = g02 * grad_x + g12 * grad_y + g22 * grad_z
                x_high, x_low = split(flux_x)
                y_high, y_low = split(flux_y)
                z_high, z_low = split(flux_z)
                twice = product(back_xy, jnp.concatenate([x_high, y_high, x_low, y_low], axis=0))
                terms = twice[:64] + twice[64:]
                weight = jnp.concatenate([scale[0:64, :]] * (STEP // LANES), axis=1)
                terms = terms + weight * along_lanes(z_high, z_low, back_z)
                terms = terms.reshape(8, 8, STEP)
                local[comp, :, :, lanes] = terms
                for n in range(8):
                    y_out[0, comp, n : n + 1, lanes] = terms[n, 7:8]
                    y_out[1, comp, n : n + 1, lanes] = terms[n, 0:1]
        if at == 0:
            pl.semaphore_wait(barrier, greeted)
        for side in range(2):
            when_do(target("gx", side), lambda: x_copy(side, c).start())
            when_do(target("gy", side), lambda: y_copy(side, c).start())

    for c in order:
        lanes = slice(c * chunk, (c + 1) * chunk)
        for side in range(2):
            when_do(source("gx", side), lambda: x_copy(side, c).wait_recv())
        for side in range(2):
            row = 7 if side == 0 else 0
            for comp in range(comps):
                for x_side in range(2):
                    at_row = 2 * comp + x_side
                    corner_out[side, at_row : at_row + 1, lanes] = x_in[
                        x_side, comp, row : row + 1, lanes
                    ]
            when_do(target("gy", side), lambda: c_copy(side, c).start())

    sub = lax.broadcasted_iota(jnp.int32, (8, LANES), 0)

    def xy_sum(comp, n, lanes):
        value = local[comp, n, :, lanes]
        from_below = y_in[0, comp, n : n + 1, lanes]
        from_above = y_in[1, comp, n : n + 1, lanes]
        if n in (0, 7):
            x_side = 0 if n == 0 else 1
            at_row = 2 * comp + x_side
            value = value + x_in[x_side, comp, :, lanes]
            from_below = from_below + corner_in[0, at_row : at_row + 1, lanes]
            from_above = from_above + corner_in[1, at_row : at_row + 1, lanes]
        where = lax.broadcasted_iota(jnp.int32, value.shape, 0)
        value = value + jnp.where(where == 0, from_below, 0.0)
        return value + jnp.where(where == 7, from_above, 0.0)

    def arrived(c):
        for side in range(2):
            when_do(source("gy", side), lambda: y_copy(side, c).wait_recv())
            when_do(source("gy", side), lambda: c_copy(side, c).wait_recv())

    edge = order[:2] if count > 1 else order
    for c in edge:
        arrived(c)
    for side in range(2):
        lanes = slice(total - LANES, total) if side == 0 else slice(0, LANES)
        for comp in range(comps):
            for n in range(8):
                z_out[side, comp, n] = xy_sum(comp, n, lanes)
        when_do(target("gz", side), lambda: z_copy(side).start())

    for c in order[len(edge) :]:
        arrived(c)
    for side in range(2):
        when_do(source("gz", side), lambda: z_copy(side).wait_recv())

    for comp in range(comps):
        for n in range(8):
            value = xy_sum(comp, n, slice(0, total))
            left = jnp.concatenate(
                [z_in[0, comp, n], value, z_in[1, comp, n]], axis=1
            )
            width = left.shape[1]
            before = pltpu.roll(left, 1, 1)[:, LANES : LANES + total]
            after = pltpu.roll(left, width - 1, 1)[:, LANES : LANES + total]
            position = lax.broadcasted_iota(jnp.int32, value.shape, 1) % 8
            extra = jnp.where(position == 7, after, jnp.where(position == 0, before, 0.0))
            out[comp, n] = value + extra

    for c in order:
        for side in range(2):
            when_do(target("gx", side), lambda: x_copy(side, c).wait_send())
            when_do(target("gy", side), lambda: y_copy(side, c).wait_send())
            when_do(target("gy", side), lambda: c_copy(side, c).wait_send())
    for side in range(2):
        when_do(target("gz", side), lambda: z_copy(side).wait_send())


def local_part(sizes, nodal_scalar_values, geometry):
    comps, _, _, total = nodal_scalar_values.shape
    chunk = min(512, total)
    count = total // chunk
    matrices, scales = tables()
    f32 = jnp.float32
    dma = pltpu.SemaphoreType.DMA
    any_space = pl.BlockSpec(memory_space=pl.ANY)
    return pl.pallas_call(
        functools.partial(kernel, sizes, chunk),
        out_shape=jax.ShapeDtypeStruct(nodal_scalar_values.shape, f32),
        in_specs=[any_space] * 4,
        out_specs=pl.BlockSpec(memory_space=pltpu.VMEM),
        scratch_shapes=[
            pltpu.VMEM(nodal_scalar_values.shape, f32),
            pltpu.VMEM(geometry.shape, f32),
            pltpu.VMEM(matrices.shape, jnp.bfloat16),
            pltpu.VMEM(scales.shape, f32),
            pltpu.VMEM((8, total), f32),
            pltpu.VMEM(nodal_scalar_values.shape, f32),
            pltpu.VMEM((2, comps, 8, total), f32),
            pltpu.VMEM((2, comps, 8, total), f32),
            pltpu.VMEM((2, comps, 8, total), f32),
            pltpu.VMEM((2, 8, total), f32),
            pltpu.VMEM((2, 8, total), f32),
            pltpu.VMEM((2, comps, 8, 8, LANES), f32),
            pltpu.VMEM((2, comps, 8, 8, LANES), f32),
            dma((count,)),
            dma((3,)),
            dma((2, count)),
            dma((2, count)),
            dma((2, count)),
            dma((2, count)),
            dma((2, count)),
            dma((2, count)),
            dma((2,)),
            dma((2,)),
        ],
        compiler_params=pltpu.CompilerParams(collective_id=0, has_side_effects=True),
        name="poisson",
    )(nodal_scalar_values, geometry, jnp.asarray(matrices), jnp.asarray(scales))


def solution(mesh):
    return jax.shard_map(
        functools.partial(local_part, dict(mesh.shape)),
        mesh=mesh,
        in_specs=(P(None, "gx", "gy", "gz"), P(None, "gx", "gy", "gz")),
        out_specs=P(None, "gx", "gy", "gz"),
        check_vma=False,
    )
```

time: 72.1 us -> 23.9 us (0.33)
  the two profiles are of different devices: /device:TPU:29 before, /device:TPU:0 now
where the time goes in v1:
time: 23.9 us; the launch traced here: 23.8 us
  Pallas kernels  21 us (88%)
  local copies, waits for them, and re-layouts  2.7 us (11%)
    pallas_call x1, Pallas kernels, local_part(): pl.pallas_call(functools.partial(kernel, sizes, chunk), out_shape=jax.Sha...  21 us
    unnamed x1, local copies, waits for them, and re-layouts  2.7 us

profile of v1, /device:TPU:0, one launch (start us, length us, event | category | flops | bytes accessed | tf_op | source)
XLA Modules:
  0.0 23.8 jit_solution(6322486828977367106)
XLA Ops:
  0.0 21.0 %poisson.1 = f32[3,8,8,2048]{3,2,1,0:T(8,128)} custom-call(f32[3,8,8,2048]{3,2,1,0:T(8,128)} %u_hbm.1, f32[6,1,1,256]{3,2,1,0:T(1,128)} %geo_hbm.1, bf16[768,256]{1,0:T(8,128)(2,1)} %constant.4.clone.mat_hbm, f32[72,128]{1,0:T(8,128)} %constant.5.clone.scale_hbm), custom_call_target="tpu_custom_call" | custom-call | tf_op jit(solution)/shard_map/poisson/pallas_call | solution.py:370
  21.1 2.7 %copy.6 = f32[3,8,8,2048]{3,2,1,0:T(8,128)} copy(f32[3,8,8,2048]{3,2,1,0:T(8,128)} %poisson.1) | data formatting | bytes 3145728

commit v2 on v1

--- a/solution.py
+++ b/solution.py
@@ -19,6 +19,8 @@
 MESH = pl.DeviceIdType.MESH
 STEP = 256
 LANES = 128
+X_FIRST = True
+LAG = 4
 
 
 def legendre_seven(point):
@@ -82,6 +84,14 @@
     return matrices, scales
 
 
+def seat(comp, m):
+    if m in (0, 7):
+        return 0, 2 * comp + (1 if m == 7 else 0)
+    if comp:
+        return comp, m - 1
+    return (m - 1) // 2, 6 + (m - 1) % 2
+
+
 def split(value):
     high = value.astype(jnp.bfloat16)
     low = (value - high.astype(jnp.float32)).astype(jnp.bfloat16)
@@ -117,6 +127,7 @@
     scale,
     metric,
     local,
+    x_out,
     y_out,
     x_in,
     y_in,
@@ -124,6 +135,7 @@
     corner_in,
     z_out,
     z_in,
+    relay,
     in_sem,
     const_sem,
     x_send,
@@ -134,6 +146,10 @@
     c_recv,
     z_send,
     z_recv,
+    r_send,
+    r_recv,
+    b_send,
+    b_recv,
 ):
     comps, _, _, total = u.shape
     count = total // chunk
@@ -168,6 +184,12 @@
                     barrier, inc=1, device_id={name: place[name] + by}, device_id_type=MESH
                 )
 
+    detour = sizes["gx"] == 4
+    relayed = order[: count * 3 // 4] if detour else []
+    opposite = lax.rem(place["gx"] + 2, 4)
+    if detour:
+        pl.semaphore_signal(barrier, inc=1, device_id={"gx": opposite}, device_id_type=MESH)
+
     for side in range(2):
         there = below if side == 0 else above
 
@@ -200,13 +222,69 @@
     def x_copy(side, c):
         span = pl.ds(c * chunk, chunk)
         return pltpu.make_async_remote_copy(
-            local.at[:, 7 if side == 0 else 0, :, span],
-            x_in.at[side, :, :, span],
+            x_out.at[side, 0, :, span],
+            x_in.at[side, 0, :, span],
             x_send.at[side, c],
             x_recv.at[side, c],
             device_id={"gx": place["gx"] + (1 if side == 0 else -1)},
             device_id_type=MESH,
         )
+
+    def bulk_copy(side, c):
+        span = pl.ds(c * chunk, chunk)
+        return pltpu.make_async_remote_copy(
+            x_out.at[side, 1:, :, span],
+            x_in.at[side, 1:, :, span],
+            b_send.at[side, c],
+            b_recv.at[side, c],
+            device_id={"gx": place["gx"] + (1 if side == 0 else -1)},
+            device_id_type=MESH,
+        )
+
+    def middle(side):
+        return place["gx"] == 1 + side
+
+    def by_way_of(side):
+        return 3 * (1 - side) if X_FIRST else 3 * side
+
+    def hop_copy(side, c):
+        span = pl.ds(c * chunk, chunk)
+        return pltpu.make_async_remote_copy(
+            x_out.at[side, 1:, :, span],
+            relay.at[:, :, span],
+            b_send.at[side, c],
+            r_recv.at[c],
+            device_id={"gx": by_way_of(side)},
+            device_id_type=MESH,
+        )
+
+    def onward_copy(side, c):
+        span = pl.ds(c * chunk, chunk)
+        return pltpu.make_async_remote_copy(
+            relay.at[:, :, span],
+            x_in.at[side, 1:, :, span],
+            r_send.at[c],
+            b_recv.at[side, c],
+            device_id={"gx": 2 - side},
+            device_id_type=MESH,
+        )
+
+    def forward(c):
+        for side in range(2):
+
+            @pl.when(place["gx"] == by_way_of(side))
+            def _(side=side):
+                hop_copy(side, c).wait_recv()
+                onward_copy(side, c).start()
+
+    def send_bulk(c):
+        for side in range(2):
+            if c in relayed:
+                straight = jnp.logical_and(target("gx", side), jnp.logical_not(middle(side)))
+                when_do(straight, lambda: bulk_copy(side, c).start())
+                when_do(middle(side), lambda: hop_copy(side, c).start())
+            else:
+                when_do(target("gx", side), lambda: bulk_copy(side, c).start())
 
     def y_copy(side, c):
         span = pl.ds(c * chunk, chunk)
@@ -251,10 +329,26 @@
         def _():
             act()
 
+    def corners(c):
+        lanes = slice(c * chunk, (c + 1) * chunk)
+        for side in range(2):
+            when_do(source("gx", side), lambda: x_copy(side, c).wait_recv())
+        for side in range(2):
+            for comp in range(comps):
+                for x_side in range(2):
+                    at_row = 2 * comp + x_side
+                    tile, row = seat(comp, 7 if side == 0 else 0)
+                    corner_out[side, at_row : at_row + 1, lanes] = x_in[
+                        x_side, tile, row : row + 1, lanes
+                    ]
+            when_do(target("gy", side), lambda: c_copy(side, c).start())
+
     forward_xy, back_xy = mat[0:128, :], mat[128:256, :]
     forward_z, back_z = mat[256:512, :], mat[512:768, :]
 
     greeted = sum(side[name].astype(jnp.int32) for name in names for side in (below, above))
+    greeted = greeted + (1 if detour else 0)
+    waiting, cornering = list(relayed), list(order)
     for at, c in enumerate(order):
         in_copies[c].wait()
         for start in range(c * chunk, (c + 1) * chunk, STEP):
@@ -281,27 +375,26 @@
                 for n in range(8):
                     y_out[0, comp, n : n + 1, lanes] = terms[n, 7:8]
                     y_out[1, comp, n : n + 1, lanes] = terms[n, 0:1]
+                    tile, row = seat(comp, n)
+                    x_out[0, tile, row : row + 1, lanes] = terms[7, n : n + 1]
+                    x_out[1, tile, row : row + 1, lanes] = terms[0, n : n + 1]
         if at == 0:
             pl.semaphore_wait(barrier, greeted)
         for side in range(2):
             when_do(target("gx", side), lambda: x_copy(side, c).start())
             when_do(target("gy", side), lambda: y_copy(side, c).start())
-
-    for c in order:
-        lanes = slice(c * chunk, (c + 1) * chunk)
-        for side in range(2):
-            when_do(source("gx", side), lambda: x_copy(side, c).wait_recv())
-        for side in range(2):
-            row = 7 if side == 0 else 0
-            for comp in range(comps):
-                for x_side in range(2):
-                    at_row = 2 * comp + x_side
-                    corner_out[side, at_row : at_row + 1, lanes] = x_in[
-                        x_side, comp, row : row + 1, lanes
-                    ]
-            when_do(target("gy", side), lambda: c_copy(side, c).start())
-
-    sub = lax.broadcasted_iota(jnp.int32, (8, LANES), 0)
+        if at:
+            send_bulk(order[at - 1])
+        if at >= LAG and cornering:
+            corners(cornering.pop(0))
+        if at >= LAG + 1 and waiting:
+            forward(waiting.pop(0))
+    send_bulk(order[-1])
+    while waiting or cornering:
+        if cornering:
+            corners(cornering.pop(0))
+        if waiting:
+            forward(waiting.pop(0))
 
     def xy_sum(comp, n, lanes):
         value = local[comp, n, :, lanes]
@@ -310,7 +403,9 @@
         if n in (0, 7):
             x_side = 0 if n == 0 else 1
             at_row = 2 * comp + x_side
-            value = value + x_in[x_side, comp, :, lanes]
+            seats = [seat(comp, m) for m in range(8)]
+            rows = [x_in[x_side, tile, row : row + 1, lanes] for tile, row in seats]
+            value = value + jnp.concatenate(rows, axis=0)
             from_below = from_below + corner_in[0, at_row : at_row + 1, lanes]
             from_above = from_above + corner_in[1, at_row : at_row + 1, lanes]
         where = lax.broadcasted_iota(jnp.int32, value.shape, 0)
@@ -319,49 +414,66 @@
 
     def arrived(c):
         for side in range(2):
+            when_do(source("gx", side), lambda: bulk_copy(side, c).wait_recv())
             when_do(source("gy", side), lambda: y_copy(side, c).wait_recv())
             when_do(source("gy", side), lambda: c_copy(side, c).wait_recv())
 
-    edge = order[:2] if count > 1 else order
-    for c in edge:
-        arrived(c)
-    for side in range(2):
-        lanes = slice(total - LANES, total) if side == 0 else slice(0, LANES)
+    def finish(first, last):
         for comp in range(comps):
             for n in range(8):
-                z_out[side, comp, n] = xy_sum(comp, n, lanes)
-        when_do(target("gz", side), lambda: z_copy(side).start())
-
-    for c in order[len(edge) :]:
+                value = xy_sum(comp, n, slice(max(first - LANES, 0), min(last + LANES, total)))
+                if first == 0:
+                    value = jnp.concatenate([z_in[0, comp, n], value], axis=1)
+                if last == total:
+                    value = jnp.concatenate([value, z_in[1, comp, n]], axis=1)
+                width = value.shape[1]
+                before = pltpu.roll(value, 1, 1)[:, LANES:-LANES]
+                after = pltpu.roll(value, width - 1, 1)[:, LANES:-LANES]
+                position = lax.broadcasted_iota(jnp.int32, before.shape, 1) % 8
+                extra = jnp.where(position == 7, after, jnp.where(position == 0, before, 0.0))
+                out[comp, n, :, first:last] = value[:, LANES:-LANES] + extra
+
+    edge = order[:2] if count > 1 else order
+    group = min(2 * chunk, total)
+    groups = list(range(total // group))
+    here = set()
+    z_here = False
+    for at, c in enumerate(order):
         arrived(c)
-    for side in range(2):
-        when_do(source("gz", side), lambda: z_copy(side).wait_recv())
-
-    for comp in range(comps):
-        for n in range(8):
-            value = xy_sum(comp, n, slice(0, total))
-            left = jnp.concatenate(
-                [z_in[0, comp, n], value, z_in[1, comp, n]], axis=1
-            )
-            width = left.shape[1]
-            before = pltpu.roll(left, 1, 1)[:, LANES : LANES + total]
-            after = pltpu.roll(left, width - 1, 1)[:, LANES : LANES + total]
-            position = lax.broadcasted_iota(jnp.int32, value.shape, 1) % 8
-            extra = jnp.where(position == 7, after, jnp.where(position == 0, before, 0.0))
-            out[comp, n] = value + extra
+        here.add(c)
+        if at == len(edge) - 1:
+            for side in range(2):
+                lanes = slice(total - LANES, total) if side == 0 else slice(0, LANES)
+                for comp in range(comps):
+                    for n in range(8):
+                        z_out[side, comp, n] = xy_sum(comp, n, lanes)
+                when_do(target("gz", side), lambda: z_copy(side).start())
+        for g in list(groups):
+            first, last = g * group // chunk, (g + 1) * group // chunk
+            if all(i in here for i in range(max(first - 1, 0), min(last + 1, count))):
+                groups.remove(g)
+                ends = g * group, (g + 1) * group
+                if not z_here and (ends[0] == 0 or ends[1] == total):
+                    z_here = True
+                    for side in range(2):
+                        when_do(source("gz", side), lambda: z_copy(side).wait_recv())
+                finish(*ends)
 
     for c in order:
         for side in range(2):
             when_do(target("gx", side), lambda: x_copy(side, c).wait_send())
+            when_do(target("gx", side), lambda: bulk_copy(side, c).wait_send())
             when_do(target("gy", side), lambda: y_copy(side, c).wait_send())
             when_do(target("gy", side), lambda: c_copy(side, c).wait_send())
     for side in range(2):
         when_do(target("gz", side), lambda: z_copy(side).wait_send())
+        for c in relayed:
+            when_do(place["gx"] == by_way_of(side), lambda: onward_copy(side, c).wait_send())
 
 
 def local_part(sizes, nodal_scalar_values, geometry):
     comps, _, _, total = nodal_scalar_values.shape
-    chunk = min(512, total)
+    chunk = min(256, total)
     count = total // chunk
     matrices, scales = tables()
     f32 = jnp.float32
@@ -369,7 +481,7 @@
     any_space = pl.BlockSpec(memory_space=pl.ANY)
     return pl.pallas_call(
         functools.partial(kernel, sizes, chunk),
-        out_shape=jax.ShapeDtypeStruct(nodal_scalar_values.shape, f32),
+        out_shape=pltpu.VMEM(nodal_scalar_values.shape, f32),
         in_specs=[any_space] * 4,
         out_specs=pl.BlockSpec(memory_space=pltpu.VMEM),
         scratch_shapes=[
@@ -382,10 +494,12 @@
             pltpu.VMEM((2, comps, 8, total), f32),
             pltpu.VMEM((2, comps, 8, total), f32),
             pltpu.VMEM((2, comps, 8, total), f32),
+            pltpu.VMEM((2, comps, 8, total), f32),
             pltpu.VMEM((2, 8, total), f32),
             pltpu.VMEM((2, 8, total), f32),
             pltpu.VMEM((2, comps, 8, 8, LANES), f32),
             pltpu.VMEM((2, comps, 8, 8, LANES), f32),
+            pltpu.VMEM((comps - 1, 8, total), f32),
             dma((count,)),
             dma((3,)),
             dma((2, count)),
@@ -396,6 +510,10 @@
             dma((2, count)),
             dma((2,)),
             dma((2,)),
+            dma((count,)),
+            dma((count,)),
+            dma((2, count)),
+            dma((2, count)),
         ],
         compiler_params=pltpu.CompilerParams(collective_id=0, has_side_effects=True),
         name="poisson",

time: 23.9 us -> 20.8 us (0.87)
  local copies, waits for them, and re-layouts: 2.7 us -> 1.15 us
  Pallas kernels: 21 us -> 19.5 us
    unnamed x1, local copies, waits for them, and re-layouts: 2.7 us -> 1.15 us
    pallas_call x1, Pallas kernels: 21 us -> 19.5 us  [local_part(): pl.pallas_call(functools.partial(kernel, sizes, chunk), out_shape=pltpu.V...]
where the time goes in v2:
time: 20.8 us; the launch traced here: 20.7 us
  Pallas kernels  19.5 us (94%)
  local copies, waits for them, and re-layouts  1.15 us (6%)
    pallas_call x1, Pallas kernels, local_part(): pl.pallas_call(functools.partial(kernel, sizes, chunk), out_shape=pltpu.V...  19.5 us
    unnamed x1, local copies, waits for them, and re-layouts  1.15 us

profile of v2, /device:TPU:0, one launch (start us, length us, event | category | flops | bytes accessed | tf_op | source)
XLA Modules:
  0.0 20.7 jit_solution(8216127469500107318)
XLA Ops:
  0.0 19.5 %poisson.1 = f32[3,8,8,2048]{3,2,1,0:T(8,128)S(1)} custom-call(f32[3,8,8,2048]{3,2,1,0:T(8,128)} %u_hbm.1, f32[6,1,1,256]{3,2,1,0:T(1,128)} %geo_hbm.1, bf16[768,256]{1,0:T(8,128)(2,1)} %constant.4.clone.mat_hbm, f32[72,128]{1,0:T(8,128)} %constant.5.clone.scale_hbm), custom_call_target="tpu_custom_call" | custom-call | tf_op jit(solution)/shard_map/poisson/pallas_call | solution.py:482
  19.5 1.1 %copy.6 = f32[3,8,8,2048]{3,2,1,0:T(8,128)} copy(f32[3,8,8,2048]{3,2,1,0:T(8,128)S(1)} %poisson.1) | data formatting | bytes 3145728

commit v3 on v2

--- a/solution.py
+++ b/solution.py
@@ -20,7 +20,7 @@
 STEP = 256
 LANES = 128
 X_FIRST = True
-LAG = 4
+LAG = 5
 
 
 def legendre_seven(point):
@@ -102,15 +102,21 @@
     return jnp.dot(left, right, preferred_element_type=jnp.float32)
 
 
-def along_lanes(high, low, table):
-    pieces = []
-    for start in range(0, high.shape[1], LANES):
-        both = jnp.concatenate(
-            [high[:, start : start + LANES], low[:, start : start + LANES]], axis=1
-        )
-        twice = product(both, table)
-        pieces.append(twice[:, :LANES] + twice[:, LANES:])
-    return jnp.concatenate(pieces, axis=1)
+def along_lanes(pairs, table):
+    rows, width = pairs[0][0].shape
+    spans = [slice(start, start + LANES) for start in range(0, width, LANES)]
+    stacked = [
+        jnp.concatenate([high[:, span], low[:, span]], axis=1)
+        for high, low in pairs
+        for span in spans
+    ]
+    twice = product(jnp.concatenate(stacked, axis=0), table)
+    once = twice[:, :LANES] + twice[:, LANES:]
+    pieces = [once[at * rows : (at + 1) * rows] for at in range(len(stacked))]
+    return [
+        jnp.concatenate(pieces[at : at + len(spans)], axis=1)
+        for at in range(0, len(pieces), len(spans))
+    ]
 
 
 def kernel(
@@ -354,22 +360,28 @@
         for start in range(c * chunk, (c + 1) * chunk, STEP):
             lanes = slice(start, start + STEP)
             g00, g11, g22, g01, g02, g12 = [metric[k : k + 1, lanes] for k in range(6)]
-            for comp in range(comps):
-                field = u[comp, :, :, lanes].reshape(64, STEP)
-                high, low = split(field)
-                both = product(forward_xy, jnp.concatenate([high, low, high, low], axis=0))
+            pairs = [split(u[comp, :, :, lanes].reshape(64, STEP)) for comp in range(comps)]
+            planes = [
+                product(forward_xy, jnp.concatenate([high, low, high, low], axis=0))
+                for high, low in pairs
+            ]
+            grads_z = along_lanes(pairs, forward_z)
+            sums, z_pairs = [], []
+            for both, grad_z in zip(planes, grads_z):
                 grad_x, grad_y = both[:64], both[64:]
-                grad_z = along_lanes(high, low, forward_z)
                 flux_x = g00 * grad_x + g01 * grad_y + g02 * grad_z
                 flux_y = g01 * grad_x + g11 * grad_y + g12 * grad_z
-                flux_z = g02 * grad_x + g12 * grad_y + g22 * grad_z
                 x_high, x_low = split(flux_x)
                 y_high, y_low = split(flux_y)
-                z_high, z_low = split(flux_z)
-                twice = product(back_xy, jnp.concatenate([x_high, y_high, x_low, y_low], axis=0))
-                terms = twice[:64] + twice[64:]
-                weight = jnp.concatenate([scale[0:64, :]] * (STEP // LANES), axis=1)
-                terms = terms + weight * along_lanes(z_high, z_low, back_z)
+                z_pairs.append(split(g02 * grad_x + g12 * grad_y + g22 * grad_z))
+                sums.append(
+                    product(back_xy, jnp.concatenate([x_high, y_high, x_low, y_low], axis=0))
+                )
+            backs_z = along_lanes(z_pairs, back_z)
+            weight = jnp.concatenate([scale[0:64, :]] * (STEP // LANES), axis=1)
+            for comp in range(comps):
+                twice = sums[comp]
+                terms = twice[:64] + twice[64:] + weight * backs_z[comp]
                 terms = terms.reshape(8, 8, STEP)
                 local[comp, :, :, lanes] = terms
                 for n in range(8):
@@ -383,13 +395,14 @@
         for side in range(2):
             when_do(target("gx", side), lambda: x_copy(side, c).start())
             when_do(target("gy", side), lambda: y_copy(side, c).start())
-        if at:
-            send_bulk(order[at - 1])
+        if at > 1:
+            send_bulk(order[at - 2])
         if at >= LAG and cornering:
             corners(cornering.pop(0))
         if at >= LAG + 1 and waiting:
             forward(waiting.pop(0))
-    send_bulk(order[-1])
+    for c in order[-2:]:
+        send_bulk(c)
     while waiting or cornering:
         if cornering:
             corners(cornering.pop(0))

time: 20.8 us -> 18.1 us (0.87)
  Pallas kernels: 19.5 us -> 16.8 us
    pallas_call x1, Pallas kernels: 19.5 us -> 16.8 us  [local_part(): pl.pallas_call(functools.partial(kernel, sizes, chunk), out_shape=pltpu.V...]
where the time goes in v3:
time: 18.1 us; the launch traced here: 18 us
  Pallas kernels  16.8 us (93%)
  local copies, waits for them, and re-layouts  1.15 us (6%)
    pallas_call x1, Pallas kernels, local_part(): pl.pallas_call(functools.partial(kernel, sizes, chunk), out_shape=pltpu.V...  16.8 us
    unnamed x1, local copies, waits for them, and re-layouts  1.15 us

profile of v3, /device:TPU:0, one launch (start us, length us, event | category | flops | bytes accessed | tf_op | source)
XLA Modules:
  0.0 18.0 jit_solution(10843800737384420421)
XLA Ops:
  0.0 16.8 %poisson.1 = f32[3,8,8,2048]{3,2,1,0:T(8,128)S(1)} custom-call(f32[3,8,8,2048]{3,2,1,0:T(8,128)} %u_hbm.1, f32[6,1,1,256]{3,2,1,0:T(1,128)} %geo_hbm.1, bf16[768,256]{1,0:T(8,128)(2,1)} %constant.4.clone.mat_hbm, f32[72,128]{1,0:T(8,128)} %constant.5.clone.scale_hbm), custom_call_target="tpu_custom_call" | custom-call | tf_op jit(solution)/shard_map/poisson/pallas_call | solution.py:495
  16.9 1.1 %copy.6 = f32[3,8,8,2048]{3,2,1,0:T(8,128)} copy(f32[3,8,8,2048]{3,2,1,0:T(8,128)S(1)} %poisson.1) | data formatting | bytes 3145728

commit v4 on v3

--- a/solution.py
+++ b/solution.py
@@ -395,13 +395,13 @@
         for side in range(2):
             when_do(target("gx", side), lambda: x_copy(side, c).start())
             when_do(target("gy", side), lambda: y_copy(side, c).start())
-        if at > 1:
-            send_bulk(order[at - 2])
+        if at > 2:
+            send_bulk(order[at - 3])
         if at >= LAG and cornering:
             corners(cornering.pop(0))
         if at >= LAG + 1 and waiting:
             forward(waiting.pop(0))
-    for c in order[-2:]:
+    for c in order[-3:]:
         send_bulk(c)
     while waiting or cornering:
         if cornering:

time: 18.1 us -> 18 us (level)
  no operation moved by 1% of the time
where the time goes in v4:
time: 18 us; the launch traced here: 17.9 us
  Pallas kernels  16.8 us (93%)
  local copies, waits for them, and re-layouts  1.15 us (6%)
    pallas_call x1, Pallas kernels, local_part(): pl.pallas_call(functools.partial(kernel, sizes, chunk), out_shape=pltpu.V...  16.8 us
    unnamed x1, local copies, waits for them, and re-layouts  1.15 us

profile of v4, /device:TPU:0, one launch (start us, length us, event | category | flops | bytes accessed | tf_op | source)
XLA Modules:
  0.0 17.9 jit_solution(15949467979972441722)
XLA Ops:
  0.0 16.8 %poisson.1 = f32[3,8,8,2048]{3,2,1,0:T(8,128)S(1)} custom-call(f32[3,8,8,2048]{3,2,1,0:T(8,128)} %u_hbm.1, f32[6,1,1,256]{3,2,1,0:T(1,128)} %geo_hbm.1, bf16[768,256]{1,0:T(8,128)(2,1)} %constant.4.clone.mat_hbm, f32[72,128]{1,0:T(8,128)} %constant.5.clone.scale_hbm), custom_call_target="tpu_custom_call" | custom-call | tf_op jit(solution)/shard_map/poisson/pallas_call | solution.py:495
  16.8 1.1 %copy.6 = f32[3,8,8,2048]{3,2,1,0:T(8,128)} copy(f32[3,8,8,2048]{3,2,1,0:T(8,128)S(1)} %poisson.1) | data formatting | bytes 3145728
